TPU v7x, 512 devices: a whole 4x8x8 slice. The times are simulated.
512 devices in a mesh: head: 2 (over core), ctx: 256 (over z, y, x).
Axes of the slice: x: 4, y: 8, z: 8, core: 2. Of those that a mesh axis runs over, the one named last changes fastest.
Arguments:
- queries: bfloat16 [65536, 4096], P(('ctx', 'head')), may hold values from -6 to 6
- keys: bfloat16 [65536, 512], P(('ctx', 'head')), may hold values from -6 to 6
- values: bfloat16 [65536, 512], P(('ctx', 'head')), may hold values from -6 to 6
- attn_out: bfloat16 [65536, 4096], P(('ctx', 'head')), may hold values from -6 to 6
- output_gradient: bfloat16 [65536, 4096], P(('ctx', 'head')), may hold values from -6 to 6
- doc_lengths: int32 [512], replicated, may hold values from 1 to 257, 65536 in all
Outputs:
- query_grad: bfloat16 [65536, 4096], P(('ctx', 'head'))
- key_gradient: bfloat16 [65536, 512], P(('ctx', 'head'))
- value_gradient: bfloat16 [65536, 512], P(('ctx', 'head'))
Inputs may be any that keep to these rules, and one draw needn't show every extreme that they name: `doc_lengths`: documents fill the 65536 tokens in order; one document has exactly 257 tokens.
All inputs are finite; a program needn't handle non-finite values.
Results may differ from a plain program's by a relative error of at most 0.0054.
Values may be sent and summed in bfloat16 or wider, within the bound.
No kernel may reach another device: no remote copies, remote signals or barrier semaphores. Data moves between devices by JAX's collectives and lax.ppermute only.
A program may use at most 64 MiB of HBM per device.

v0:
```python
import jax
import jax.numpy as jnp
from jax import lax
from jax.sharding import PartitionSpec as P

QUERY_HEAD_COUNT = 32
KEY_VALUE_HEADS = 4
HEAD_SIZE = 128
REACH = 1


fill_value = -1e30


def shifted(shard, axis, by):
    size = lax.axis_size(axis)
    pairs = [(i, i + by) for i in range(size) if 0 <= i + by < size]
    return lax.ppermute(shard, axis, pairs)


def segment_ids(doc_lengths, positions):
    ends = jnp.cumsum(doc_lengths)
    found = jnp.sum(
        (ends[None, :] <= positions[:, None]).astype(jnp.int32), axis=1, dtype=jnp.int32
    )
    return jnp.where(positions >= 0, found, -1)


def kv_window(key_part, value_part):
    window = [(key_part, value_part)]
    window.append(shifted((key_part, value_part), "ctx", 1))
    return window


def grad_return(key_parts, value_parts):
    key_total = key_parts[0]
    value_total = value_parts[0]
    back_key, back_value = shifted((key_parts[1], value_parts[1]), "ctx", -1)
    key_total = key_total + back_key
    value_total = value_total + back_value
    return (key_total, value_total)


def on_device(queries, keys, values, attn_out, output_gradient, doc_lengths):
    local_rows = queries.shape[0]
    group_width = QUERY_HEAD_COUNT // KEY_VALUE_HEADS
    score_scale = HEAD_SIZE ** (-0.5)
    delta_value = jnp.sum(
        (output_gradient.astype(jnp.float32) * attn_out.astype(jnp.float32)).reshape(
            local_rows, QUERY_HEAD_COUNT, HEAD_SIZE
        ),
        axis=2,
    ).astype(jnp.bfloat16)
    shard_index = lax.axis_index("ctx")
    query_side, grad_side, delta_side, key_side, value_side = (
        lax.all_to_all(queries, "head", split_axis=1, concat_axis=0, tiled=True),
        lax.all_to_all(output_gradient, "head", split_axis=1, concat_axis=0, tiled=True),
        lax.all_to_all(delta_value, "head", split_axis=1, concat_axis=0, tiled=True),
        lax.all_to_all(keys, "head", split_axis=1, concat_axis=0, tiled=True),
        lax.all_to_all(values, "head", split_axis=1, concat_axis=0, tiled=True),
    )
    first_row = shard_index * query_side.shape[0]
    window = kv_window(key_side, value_side)
    query_row_block = query_side.shape[0]
    key_rows = window[0][0].shape[0]
    kv_local = window[0][0].shape[1] // HEAD_SIZE
    query_heads = query_side.reshape(query_row_block, kv_local, group_width, HEAD_SIZE)
    grad_heads = grad_side.reshape(query_row_block, kv_local, group_width, HEAD_SIZE)
    row_delta_values = jnp.transpose(
        delta_side.reshape(query_row_block, kv_local, group_width).astype(jnp.float32), (1, 2, 0)
    )
    pos_query = first_row + jnp.arange(query_row_block, dtype=jnp.int32)
    seg_query = segment_ids(doc_lengths, pos_query)
    key_index = jnp.arange(key_rows, dtype=jnp.int32)
    bias_list = []
    live_list = []
    for offset in range(REACH + 1):
        pos_key = (shard_index - offset) * key_rows + key_index
        seg_key = segment_ids(doc_lengths, pos_key)
        allowed = (seg_query[:, None] == seg_key[None, :]) & (
            pos_key[None, :] <= pos_query[:, None]
        )
        bias_list.append(jnp.where(allowed, 0.0, fill_value).astype(jnp.float32))
        live_list.append(jnp.logical_and(seg_key[-1] == seg_query[0], seg_key[-1] >= 0))

    def tile_scores(key_tile, bias):
        key_heads = key_tile.reshape(key_rows, kv_local, HEAD_SIZE)
        return (
            jnp.einsum("tkgd,ukd->kgtu", query_heads, key_heads, preferred_element_type=jnp.float32)
            * score_scale
            + bias
        )

    stat_shape = (kv_local, group_width, query_row_block)
    row_max = jnp.full(stat_shape, fill_value, jnp.float32)
    row_sum = jnp.zeros(stat_shape, jnp.float32)
    for offset in range(REACH + 1):
        key_tile = window[offset][0]
        bias = bias_list[offset]
        masked = tile_scores(key_tile, bias)
        tile_max = jnp.max(masked, axis=-1)
        tile_sum = jnp.sum(jnp.exp(masked - tile_max[..., None]), axis=-1)
        tile_sum = jnp.where(tile_max > 0.5 * fill_value, tile_sum, 0.0)
        tile_max, tile_sum = (tile_max, tile_sum)
        new_max = jnp.maximum(row_max, tile_max)
        row_sum = row_sum * jnp.exp(row_max - new_max) + tile_sum * jnp.exp(tile_max - new_max)
        row_max = new_max
    lse = row_max + jnp.log(row_sum)
    query_total = jnp.zeros((query_row_block, kv_local, group_width, HEAD_SIZE), jnp.float32)
    key_parts = []
    value_parts = []
    for offset in range(REACH + 1):
        key_tile, value_tile = window[offset]
        bias = bias_list[offset]
        tile_key_heads = key_tile.reshape(key_rows, kv_local, HEAD_SIZE)
        value_heads = value_tile.reshape(key_rows, kv_local, HEAD_SIZE)
        probs = jnp.exp(tile_scores(key_tile, bias) - lse[..., None])
        probs_low = probs.astype(jnp.bfloat16)
        prob_grad = jnp.einsum(
            "tkgd,ukd->kgtu", grad_heads, value_heads, preferred_element_type=jnp.float32
        )
        score_grad = (probs * (prob_grad - row_delta_values[..., None])).astype(jnp.bfloat16)
        query_part = (
            jnp.einsum(
                "kgtu,ukd->tkgd", score_grad, tile_key_heads, preferred_element_type=jnp.float32
            )
            * score_scale
        )
        key_part = (
            jnp.einsum(
                "kgtu,tkgd->ukd", score_grad, query_heads, preferred_element_type=jnp.float32
            )
            * score_scale
        )
        value_part = jnp.einsum(
            "kgtu,tkgd->ukd", probs_low, grad_heads, preferred_element_type=jnp.float32
        )
        query_part, key_part, value_part = (
            query_part,
            key_part.reshape(key_rows, kv_local * HEAD_SIZE),
            value_part.reshape(key_rows, kv_local * HEAD_SIZE),
        )
        query_total = query_total + query_part
        key_parts.append(key_part)
        value_parts.append(value_part)
    query_low = query_total.reshape(query_row_block, kv_local * group_width * HEAD_SIZE).astype(
        jnp.bfloat16
    )
    key_total, value_total = grad_return(key_parts, value_parts)
    query_grad, key_gradient, value_gradient = (
        lax.all_to_all(query_low, "head", split_axis=0, concat_axis=1, tiled=True),
        lax.all_to_all(
            key_total.astype(jnp.bfloat16), "head", split_axis=0, concat_axis=1, tiled=True
        ),
        lax.all_to_all(
            value_total.astype(jnp.bfloat16), "head", split_axis=0, concat_axis=1, tiled=True
        ),
    )
    return (query_grad, key_gradient, value_gradient)


def solution(mesh):
    in_specs = (
        P(("ctx", "head"), None),
        P(("ctx", "head"), None),
        P(("ctx", "head"), None),
        P(("ctx", "head"), None),
        P(("ctx", "head"), None),
        P(),
    )
    out_specs = (P(("ctx", "head"), None), P(("ctx", "head"), None), P(("ctx", "head"), None))
    return jax.shard_map(
        on_device, mesh=mesh, in_specs=in_specs, out_specs=out_specs, check_vma=False
    )
```

profile of v0, /device:TPU:257, one launch (start us, length us, event | category | flops | bytes accessed | tf_op | source)
XLA Modules:
  0.0 97.4 jit_solution(11718200443683200921)
XLA Ops:
  0.7 1.8 %copy.212 = bf16[128,512]{0,1:T(8,128)(2,1)} copy(bf16[128,512]{1,0:T(8,128)(2,1)} %param.8) | data formatting | bytes 262144 | tf_op args[2]
  2.4 4.0 %all-to-all-start.2 = ((bf16[128,2,256]{0,2,1:T(8,128)(2,1)}), bf16[128,2,256]{0,2,1:T(8,128)(2,1)S(1)}, u32[]{:S(2)}, u32[]{:S(2)}) async-start(bf16[128,2,256]{0,2,1:T(8,128)(2,1)} %bitcast.11), calls=%async_computation.2 | async-start | bytes 262144 | tf_op jit(solution)/shard_map/all_to_all | solution.py:60
  6.4 1.7 %copy.203 = bf16[128,512]{0,1:T(8,128)(2,1)} copy(bf16[128,512]{1,0:T(8,128)(2,1)} %param.7) | data formatting | bytes 262144 | tf_op args[1]
  8.1 3.4 %all-to-all-start = ((bf16[128,2,256]{0,2,1:T(8,128)(2,1)}), bf16[128,2,256]{0,2,1:T(8,128)(2,1)S(1)}, u32[]{:S(2)}, u32[]{:S(2)}) async-start(bf16[128,2,256]{0,2,1:T(8,128)(2,1)} %bitcast), calls=%async_computation | async-start | bytes 262144 | tf_op jit(solution)/shard_map/all_to_all | solution.py:59
  11.6 3.1 %collective-permute-start.1 = (bf16[256,256]{1,0:T(8,128)(2,1)S(1)}, bf16[256,256]{1,0:T(8,128)(2,1)}, u32[]{:S(2)}, u32[]{:S(2)}) collective-permute-start(bf16[256,256]{1,0:T(8,128)(2,1)S(1)} %bitcast.161), channel_id=1, source_target_pairs={{0,1},{1,2},{2,3},{3,4},{4,5},{5,6},{6,7},{7,8},{8,9},{9,10},{10,1... | collective-permute-start | bytes 393224 | tf_op jit(solution)/shard_map/ppermute | solution.py:18
  14.8 0.8 copy.204
  15.5 3.1 %collective-permute-start = (bf16[256,256]{1,0:T(8,128)(2,1)}, bf16[256,256]{1,0:T(8,128)(2,1)}, u32[]{:S(2)}, u32[]{:S(2)}) collective-permute-start(bf16[256,256]{1,0:T(8,128)(2,1)} %bitcast.7), channel_id=1, source_target_pairs={{0,1},{1,2},{2,3},{3,4},{4,5},{5,6},{6,7},{7,8},{8,9},{9,10},{10,1... | collective-permute-start | bytes 393224 | tf_op jit(solution)/shard_map/ppermute | solution.py:18
  18.7 2.3 %copy.288 = bf16[16,2,8,2048]{3,2,0,1:T(8,128)(2,1)} copy(bf16[16,2,8,2048]{3,2,1,0:T(8,128)(2,1)} %bitcast.158) | data formatting | bytes 2097152 | tf_op jit(solution)/shard_map/all_to_all | solution.py:56
  21.0 4.2 %all-to-all-start.1 = ((bf16[128,2,2048]{2,0,1:T(8,128)(2,1)}), bf16[128,2,2048]{2,0,1:T(8,128)(2,1)S(1)}, u32[]{:S(2)}, u32[]{:S(2)}) async-start(bf16[128,2,2048]{2,0,1:T(8,128)(2,1)} %bitcast.146), calls=%async_computation.1 | async-start | bytes 2097152 | tf_op jit(solution)/shard_map/all_to_all | solution.py:56
  25.1 0.9 reshape.283
  27.3 1.1 %copy.287 = bf16[16,2,8,2048]{3,2,0,1:T(8,128)(2,1)} copy(bf16[16,2,8,2048]{3,2,1,0:T(8,128)(2,1)S(1)} %bitcast.153) | data formatting | bytes 2097152 | tf_op jit(solution)/shard_map/all_to_all | solution.py:57
  28.4 4.4 %all-to-all-start.3 = ((bf16[128,2,2048]{2,0,1:T(8,128)(2,1)}), bf16[128,2,2048]{2,0,1:T(8,128)(2,1)}, u32[]{:S(2)}, u32[]{:S(2)}) async-start(bf16[128,2,2048]{2,0,1:T(8,128)(2,1)} %bitcast.145), calls=%async_computation.3 | async-start | bytes 2097152 | tf_op jit(solution)/shard_map/all_to_all | solution.py:57
  33.1 0.8 copy.230
  33.9 1.5 %multiply_bitcast_fusion = f32[16,8,32,128]{3,1,2,0:T(8,128)S(1)} fusion(bf16[128,4096]{1,0:T(8,128)(2,1)} %param.9, bf16[128,4096]{1,0:T(8,128)(2,1)S(1)} %copy-done.6), kind=kLoop, calls=%fused_computation.17 | loop fusion | flops 1572864 | bytes 4194304
  35.7 1.2 %reduce_sum.53 = bf16[128,32]{1,0:T(8,128)(2,1)} reduce(f32[128,32,128]{2,1,0:T(8,128)S(1)} %bitcast.147, f32[]{:T(128)} %constant.14.clone.1), dimensions={2}, to_apply=%region_8.9 | reduce | flops 520192 | bytes 2105348 | tf_op jit(solution)/shard_map/reduce_sum | solution.py:48
  37.0 1.4 %copy.217 = bf16[128,32]{0,1:T(8,128)(2,1)} copy(bf16[128,32]{1,0:T(8,128)(2,1)} %reduce_sum.53) | data formatting | bytes 16384 | tf_op jit(solution)/shard_map/reduce_sum | solution.py:48
  38.4 3.4 %all-to-all-start.4 = ((bf16[128,2,16]{0,2,1:T(8,128)(2,1)}), bf16[128,2,16]{0,2,1:T(8,128)(2,1)S(1)}, u32[]{:S(2)}, u32[]{:S(2)}) async-start(bf16[128,2,16]{0,2,1:T(8,128)(2,1)} %bitcast.16), calls=%async_computation.4 | async-start | bytes 16384 | tf_op jit(solution)/shard_map/all_to_all | solution.py:58
  41.8 1.4 %copy.275 = bf16[32,8,16,128]{3,2,1,0:T(8,128)(2,1)S(1)} copy(bf16[32,8,16,128]{3,1,2,0:T(8,128)(2,1)} %bitcast.73) | data formatting | bytes 2097152
  43.3 0.8 copy.236
  44.1 0.9 convert_reduce_fusion
  45.0 0.9 and_select_fusion
  45.9 0.7 fusion.6
  46.7 2.0 %copy-done = f32[2,256,256,8]{2,1,3,0:T(8,128)} copy-done((f32[2,256,256,8]{2,1,3,0:T(8,128)}, f32[2,256,256,8]{2,1,3,0:T(8,128)S(1)}, u32[]{:S(2)}) %copy-start) | copy-done | bytes 4194328
  48.6 0.8 exponential_reduce_fusion.1
  49.5 1.0 %copy.209 = bf16[256,256]{0,1:T(8,128)(2,1)S(1)} copy(bf16[256,256]{1,0:T(8,128)(2,1)} %collective-permute-done) | data formatting | bytes 262144 | tf_op jit(solution)/shard_map/ppermute | solution.py:18
  50.6 0.8 fusion.7
  51.3 0.8 exponential_reduce_fusion
  52.2 1.7 %copy-done.1 = f32[2,256,256,8]{2,1,3,0:T(8,128)S(1)} copy-done((f32[2,256,256,8]{2,1,3,0:T(8,128)S(1)}, f32[2,256,256,8]{2,1,3,0:T(8,128)}, u32[]{:S(2)}) %copy-start.1) | copy-done | bytes 4194328
  53.9 1.1 %fusion.10 = f32[2,256,128,1]{1,2,3,0:T(8,128)S(1)} fusion(bf16[256,2,8,128]{0,3,2,1:T(8,128)(2,1)S(1)} %copy.236, f32[2,256,256,8]{2,1,3,0:T(8,128)S(1)} %copy-done.1, f32[2,8,256]{2,1,0:T(8,128)S(1)} %fusion.28, f32[256,256]{0,1:T(8,128)S(1)} %get-tuple-element.21), kind=kOutput, calls=%fused_computation.19 | convolution fusion | flops 272629760 | bytes 5783552 | tf_op jit(solution)/shard_map/kgtu,tkgd->ukd/dot_general | solution.py:135
  55.0 1.8 %fusion.8 = f32[2,256,128,1]{1,2,3,0:T(8,128)} fusion(bf16[256,2,8,128]{0,3,2,1:T(8,128)(2,1)S(1)} %copy.236, f32[2,256,256,8]{2,1,3,0:T(8,128)S(1)} %get-tuple-element.25, f32[2,8,256]{2,1,0:T(8,128)S(1)} %fusion.28, f32[256,256]{0,1:T(8,128)S(1)} %get-tuple-element.20), kind=kOutput, calls=%fused_computation.18 | convolution fusion | flops 272629760 | bytes 5783552 | tf_op jit(solution)/shard_map/kgtu,tkgd->ukd/dot_general | solution.py:135
  56.9 1.2 %fusion.3 = bf16[2,8,256,256]{2,3,1,0:T(8,128)(2,1)S(1)} fusion(f32[2,256,256,8]{2,1,3,0:T(8,128)S(1)} %copy-done.1, bf16[256,2,8,128]{0,3,2,1:T(8,128)(2,1)S(1)} %copy.236, f32[2,8,256]{2,1,0:T(8,128)S(1)} %bitcast.169, f32[2,8,256]{2,1,0:T(8,128)S(1)} %fusion.28, f32[256,256]{0,1:T(8,128)S(1)} %get-tuple-element.21, bf16[256,2,128,1]{2,1,0,3:T(2,128)(2,1)S(1)} %bitcast.159), kind=kOutput, calls=%fused_computation.5 | convolution fusion | flops 274726912 | bytes 7766016 | tf_op jit(solution)/shard_map/tkgd,ukd->kgtu/dot_general | solution.py:119
  58.1 1.3 %copy-done.3 = bf16[2,8,256,256]{2,3,1,0:T(8,128)(2,1)} copy-done((bf16[2,8,256,256]{2,3,1,0:T(8,128)(2,1)}, bf16[2,8,256,256]{2,3,1,0:T(8,128)(2,1)S(1)}, u32[]{:S(2)}) %copy-start.3) | copy-done | bytes 2097176
  59.4 2.3 %fusion.18 = f32[2,8,256,128]{3,2,1,0:T(8,128)} fusion(bf16[2,8,256,256]{2,3,1,0:T(8,128)(2,1)S(1)} %fusion.3, bf16[256,2,128,1]{2,1,0,3:T(2,128)(2,1)S(1)} %bitcast.155), kind=kOutput, calls=%fused_computation.36 | convolution fusion | flops 268435456 | bytes 4325376 | tf_op jit(solution)/shard_map/kgtu,ukd->tkgd/dot_general | solution.py:124
  61.7 1.0 %copy.222 = bf16[256,256]{0,1:T(8,128)(2,1)S(1)} copy(bf16[256,256]{1,0:T(8,128)(2,1)} %collective-permute-done.1) | data formatting | bytes 262144 | tf_op jit(solution)/shard_map/ppermute | solution.py:18
  62.7 3.6 %fusion.1 = bf16[2,8,256,256]{2,3,1,0:T(8,128)(2,1)S(1)} fusion(f32[2,256,256,8]{2,1,3,0:T(8,128)} %copy-done.2, bf16[256,2,128,1]{0,2,3,1:T(8,128)(2,1)S(1)} %bitcast.160, bf16[256,2,8,128]{0,3,2,1:T(8,128)(2,1)S(1)} %copy.236, f32[2,8,256]{2,1,0:T(8,128)S(1)} %bitcast.170, f32[2,8,256]{2,1,0:T(8,128)S(1)} %fusion.28, f32[256,256]{0,1:T(8,128)S(1)} %get-tuple-element.20), kind=kOutput, calls=%fused_computation.2 | convolution fusion | flops 274726912 | bytes 7766016 | tf_op jit(solution)/shard_map/tkgd,ukd->kgtu/dot_general | solution.py:119
  66.4 1.5 %fusion.13 = f32[2,256,128]{1,2,0:T(8,128)} fusion(bf16[2,8,256,256]{2,3,1,0:T(8,128)(2,1)S(1)} %fusion.1, bf16[256,2,8,128]{0,3,2,1:T(8,128)(2,1)S(1)} %copy.230), kind=kOutput, calls=%fused_computation.22 | convolution fusion | flops 268500992 | bytes 3407872 | tf_op jit(solution)/shard_map/kgtu,tkgd->ukd/dot_general | solution.py:130
  67.9 1.0 fusion.12
  68.9 7.6 %collective-permute-start.3 = (f32[256,256]{0,1:T(8,128)S(1)}, f32[256,256]{0,1:T(8,128)S(1)}, u32[]{:S(2)}, u32[]{:S(2)}) collective-permute-start(f32[256,256]{0,1:T(8,128)S(1)} %bitcast.168), channel_id=1, source_target_pairs={{1,0},{2,1},{3,2},{4,3},{5,4},{6,5},{7,6},{8,7},{9,8},{10,9},{11,1... | collective-permute-start | bytes 786440 | tf_op jit(solution)/shard_map/ppermute | solution.py:18
  76.5 2.4 %collective-permute-start.2 = (f32[256,256]{0,1:T(8,128)}, f32[256,256]{0,1:T(8,128)S(1)}, u32[]{:S(2)}, u32[]{:S(2)}) collective-permute-start(f32[256,256]{0,1:T(8,128)} %bitcast.35), channel_id=1, source_target_pairs={{1,0},{2,1},{3,2},{4,3},{5,4},{6,5},{7,6},{8,7},{9,8},{10,9},{11,1... | collective-permute-start | bytes 786440 | tf_op jit(solution)/shard_map/ppermute | solution.py:18
  78.9 0.8 fusion.14
  79.7 0.7 copy.227
  80.9 4.8 %all_to_all.134 = bf16[2,128,2048]{2,1,0:T(8,128)(2,1)S(1)} all-to-all(bf16[2,128,2048]{2,1,0:T(8,128)(2,1)S(1)} %convert_element_type.67), channel_id=1, replica_groups=mesh['head'=2,'ctx'=256] {'head'}, dimensions={0} | all-to-all | bytes 2097152 | tf_op jit(solution)/shard_map/all_to_all | solution.py:151
  85.7 0.7 copy.228
  86.3 1.3 %copy.241 = bf16[128,4096]{1,0:T(8,128)(2,1)} copy(bf16[128,4096]{0,1:T(8,128)(2,1)S(1)} %bitcast.152) | data formatting | bytes 2097152
  87.8 3.9 %all_to_all.135 = bf16[2,128,256]{2,1,0:T(8,128)(2,1)S(1)} all-to-all(bf16[2,128,256]{2,1,0:T(8,128)(2,1)S(1)} %bitcast.164), channel_id=1, replica_groups=mesh['head'=2,'ctx'=256] {'head'}, dimensions={0} | all-to-all | bytes 262144 | tf_op jit(solution)/shard_map/all_to_all | solution.py:155
  91.8 0.8 copy.243
  92.7 3.8 %all_to_all.136 = bf16[2,128,256]{2,1,0:T(8,128)(2,1)S(1)} all-to-all(bf16[2,128,256]{2,1,0:T(8,128)(2,1)S(1)} %bitcast.166), channel_id=1, replica_groups=mesh['head'=2,'ctx'=256] {'head'}, dimensions={0} | all-to-all | bytes 262144 | tf_op jit(solution)/shard_map/all_to_all | solution.py:152
  96.6 0.8 copy.242
  (47 shorter events, 3.1 us)
Async XLA Ops:
  0.6 26.1 %copy-start.8 = (s32[512]{0:T(512)S(1)}, s32[512]{0:T(512)}, u32[]{:S(2)}) copy-start(s32[512]{0:T(512)} %param.11) | copy-start | bytes 6148
  0.6 26.7 %copy-start.6 = (bf16[128,4096]{1,0:T(8,128)(2,1)S(1)}, bf16[128,4096]{1,0:T(8,128)(2,1)}, u32[]{:S(2)}) copy-start(bf16[128,4096]{1,0:T(8,128)(2,1)} %param.10) | copy-start | bytes 3145732
  2.4 5.7 %all-to-all-start.2 = ((bf16[128,2,256]{0,2,1:T(8,128)(2,1)}), bf16[128,2,256]{0,2,1:T(8,128)(2,1)S(1)}, u32[]{:S(2)}, u32[]{:S(2)}) async-start(bf16[128,2,256]{0,2,1:T(8,128)(2,1)} %bitcast.11), calls=%async_computation.2 | async-start | bytes 262144 | tf_op jit(solution)/shard_map/all_to_all | solution.py:60
  8.1 6.6 %all-to-all-start = ((bf16[128,2,256]{0,2,1:T(8,128)(2,1)}), bf16[128,2,256]{0,2,1:T(8,128)(2,1)S(1)}, u32[]{:S(2)}, u32[]{:S(2)}) async-start(bf16[128,2,256]{0,2,1:T(8,128)(2,1)} %bitcast), calls=%async_computation | async-start | bytes 262144 | tf_op jit(solution)/shard_map/all_to_all | solution.py:59
  11.6 50.1 %collective-permute-start.1 = (bf16[256,256]{1,0:T(8,128)(2,1)S(1)}, bf16[256,256]{1,0:T(8,128)(2,1)}, u32[]{:S(2)}, u32[]{:S(2)}) collective-permute-start(bf16[256,256]{1,0:T(8,128)(2,1)S(1)} %bitcast.161), channel_id=1, source_target_pairs={{0,1},{1,2},{2,3},{3,4},{4,5},{5,6},{6,7},{7,8},{8,9},{9,10},{10,1... | collective-permute-start | bytes 393224 | tf_op jit(solution)/shard_map/ppermute | solution.py:18
  15.5 34.0 %collective-permute-start = (bf16[256,256]{1,0:T(8,128)(2,1)}, bf16[256,256]{1,0:T(8,128)(2,1)}, u32[]{:S(2)}, u32[]{:S(2)}) collective-permute-start(bf16[256,256]{1,0:T(8,128)(2,1)} %bitcast.7), channel_id=1, source_target_pairs={{0,1},{1,2},{2,3},{3,4},{4,5},{5,6},{6,7},{7,8},{8,9},{9,10},{10,1... | collective-permute-start | bytes 393224 | tf_op jit(solution)/shard_map/ppermute | solution.py:18
  21.0 7.5 %all-to-all-start.1 = ((bf16[128,2,2048]{2,0,1:T(8,128)(2,1)}), bf16[128,2,2048]{2,0,1:T(8,128)(2,1)S(1)}, u32[]{:S(2)}, u32[]{:S(2)}) async-start(bf16[128,2,2048]{2,0,1:T(8,128)(2,1)} %bitcast.146), calls=%async_computation.1 | async-start | bytes 2097152 | tf_op jit(solution)/shard_map/all_to_all | solution.py:56
  28.4 10.0 %all-to-all-start.3 = ((bf16[128,2,2048]{2,0,1:T(8,128)(2,1)}), bf16[128,2,2048]{2,0,1:T(8,128)(2,1)}, u32[]{:S(2)}, u32[]{:S(2)}) async-start(bf16[128,2,2048]{2,0,1:T(8,128)(2,1)} %bitcast.145), calls=%async_computation.3 | async-start | bytes 2097152 | tf_op jit(solution)/shard_map/all_to_all | solution.py:57
  38.4 11.0 %all-to-all-start.4 = ((bf16[128,2,16]{0,2,1:T(8,128)(2,1)}), bf16[128,2,16]{0,2,1:T(8,128)(2,1)S(1)}, u32[]{:S(2)}, u32[]{:S(2)}) async-start(bf16[128,2,16]{0,2,1:T(8,128)(2,1)} %bitcast.16), calls=%async_computation.4 | async-start | bytes 16384 | tf_op jit(solution)/shard_map/all_to_all | solution.py:58
  46.6 2.0 %copy-start = (f32[2,256,256,8]{2,1,3,0:T(8,128)}, f32[2,256,256,8]{2,1,3,0:T(8,128)S(1)}, u32[]{:S(2)}) copy-start(f32[2,256,256,8]{2,1,3,0:T(8,128)S(1)} %get-tuple-element.23) | copy-start | bytes 12582916
  50.5 3.4 %copy-start.1 = (f32[2,256,256,8]{2,1,3,0:T(8,128)S(1)}, f32[2,256,256,8]{2,1,3,0:T(8,128)}, u32[]{:S(2)}) copy-start(f32[2,256,256,8]{2,1,3,0:T(8,128)} %copy-done) | copy-start | bytes 12582916
  51.3 3.7 %copy-start.2 = (f32[2,256,256,8]{2,1,3,0:T(8,128)}, f32[2,256,256,8]{2,1,3,0:T(8,128)S(1)}, u32[]{:S(2)}) copy-start(f32[2,256,256,8]{2,1,3,0:T(8,128)S(1)} %get-tuple-element.25) | copy-start | bytes 12582916
  58.1 1.3 %copy-start.3 = (bf16[2,8,256,256]{2,3,1,0:T(8,128)(2,1)}, bf16[2,8,256,256]{2,3,1,0:T(8,128)(2,1)S(1)}, u32[]{:S(2)}) copy-start(bf16[2,8,256,256]{2,3,1,0:T(8,128)(2,1)S(1)} %fusion.3) | copy-start | bytes 6291460
  62.7 5.2 %copy-start.5 = (f32[2,8,256,128]{3,2,1,0:T(8,128)S(1)}, f32[2,8,256,128]{3,2,1,0:T(8,128)}, u32[]{:S(2)}) copy-start(f32[2,8,256,128]{3,2,1,0:T(8,128)} %fusion.18) | copy-start | bytes 6291460
  66.3 2.5 %copy-start.7 = (f32[2,256,128,1]{1,2,3,0:T(8,128)S(1)}, f32[2,256,128,1]{1,2,3,0:T(8,128)}, u32[]{:S(2)}) copy-start(f32[2,256,128,1]{1,2,3,0:T(8,128)} %fusion.8) | copy-start | bytes 786436
  66.4 12.5 %copy-start.4 = (bf16[2,8,256,256]{2,3,1,0:T(8,128)(2,1)S(1)}, bf16[2,8,256,256]{2,3,1,0:T(8,128)(2,1)}, u32[]{:S(2)}) copy-start(bf16[2,8,256,256]{2,3,1,0:T(8,128)(2,1)} %copy-done.3) | copy-start | bytes 6291460
  68.9 18.8 %collective-permute-start.3 = (f32[256,256]{0,1:T(8,128)S(1)}, f32[256,256]{0,1:T(8,128)S(1)}, u32[]{:S(2)}, u32[]{:S(2)}) collective-permute-start(f32[256,256]{0,1:T(8,128)S(1)} %bitcast.168), channel_id=1, source_target_pairs={{1,0},{2,1},{3,2},{4,3},{5,4},{6,5},{7,6},{8,7},{9,8},{10,9},{11,1... | collective-permute-start | bytes 786440 | tf_op jit(solution)/shard_map/ppermute | solution.py:18
  76.5 16.1 %collective-permute-start.2 = (f32[256,256]{0,1:T(8,128)}, f32[256,256]{0,1:T(8,128)S(1)}, u32[]{:S(2)}, u32[]{:S(2)}) collective-permute-start(f32[256,256]{0,1:T(8,128)} %bitcast.35), channel_id=1, source_target_pairs={{1,0},{2,1},{3,2},{4,3},{5,4},{6,5},{7,6},{8,7},{9,8},{10,9},{11,1... | collective-permute-start | bytes 786440 | tf_op jit(solution)/shard_map/ppermute | solution.py:18
where the time goes:
time: 98.5 us; the launch traced here: 97.4 us
  starting transfers between devices  35.6 us (36%)
  local copies, waits for them, and re-layouts  26.1 us (26%)
  matrix products  14.8 us (15%)
  blocking collectives  12.5 us (13%)
  other arithmetic  7.34 us (7%)
  between operations  1.06 us (1%)
    ppermute x4, starting transfers between devices, shifted(): return lax.ppermute(shard, axis, pairs)  16.2 us
    unnamed x26, local copies, waits for them, and re-layouts  13.3 us
    dot_general x2, matrix products, on_device(): jnp.einsum('tkgd,ukd->kgtu', grad_heads, value_heads, preferred_element_t...  4.82 us
    all_to_all x1, blocking collectives, on_device(): lax.all_to_all(query_low, 'head', split_axis=0, concat_axis=1, tiled=True)  4.77 us
    all_to_all x1, starting transfers between devices, on_device(): lax.all_to_all(output_gradient, 'head', split_axis=1, concat_axis=0, tile...  4.42 us
    all_to_all x1, starting transfers between devices, on_device(): lax.all_to_all(queries, 'head', split_axis=1, concat_axis=0, tiled=True)  4.15 us
    all_to_all x1, starting transfers between devices, on_device(): lax.all_to_all(values, 'head', split_axis=1, concat_axis=0, tiled=True)  4.04 us
    all_to_all x1, blocking collectives, on_device(): lax.all_to_all(value_total.astype(jnp.bfloat16), 'head', split_axis=0, co...  3.86 us
  transfers between devices with their start and end apart: 9, of which 0 were waited for; matrix products, arithmetic and copies ran while one was open for 34% of the time, Pallas kernels for 0%

commit v1 on v0

v1 whole, which is shorter than its diff:
```python
import jax
import jax.numpy as jnp
from jax import lax
from jax.experimental import pallas as pl
from jax.experimental.pallas import tpu as pltpu
from jax.sharding import PartitionSpec as P

HEADS = 32
GROUPS = 4
PER_GROUP = HEADS // GROUPS
PAIRS = PER_GROUP // 2
DIM = 128
ROWS = 128
WIDE = GROUPS * DIM
FULL = HEADS * DIM
GROUP_COLS = PER_GROUP * DIM
SCALE = DIM ** (-0.5)
LOG2E = 1.4426950408889634
TO_BITS = SCALE * LOG2E
FILL = -1e30
VMEM = pltpu.VMEM
F32 = jnp.float32
BF16 = jnp.bfloat16
NT = (((1,), (1,)), ((), ()))
NN = (((1,), (0,)), ((), ()))


def dot(a, b, dims):
    return lax.dot_general(a, b, dims, preferred_element_type=F32)


def span(start, size):
    return pl.ds(pl.multiple_of(start, DIM), size)


def stacked(ref, first, count):
    return jnp.concatenate([ref[:, span(first + i * DIM, DIM)] for i in range(count)], axis=0)


def pack_kernel(k_ref, v_ref, out_ref, sems):
    first = pltpu.make_async_copy(k_ref, out_ref.at[:, pl.ds(0, WIDE)], sems.at[0])
    second = pltpu.make_async_copy(v_ref, out_ref.at[:, pl.ds(WIDE, WIDE)], sems.at[1])
    first.start()
    second.start()
    first.wait()
    second.wait()


def local_kernel(
    pos_ref, len_hbm, q_hbm, g_hbm, o_hbm, kv_ref,
    q_ref, g_ref, start_ref, delta_ref, max_ref, sum_ref,
    len_ref, o_ref, sems, len_sem,
):
    def copies(g):
        cols = span(g * GROUP_COLS, GROUP_COLS)
        return [
            pltpu.make_async_copy(src.at[:, cols], dst.at[:, cols], sems.at[i, g])
            for i, (src, dst) in enumerate(((q_hbm, q_ref), (g_hbm, g_ref), (o_hbm, o_ref)))
        ]

    len_copy = pltpu.make_async_copy(len_hbm, len_ref, len_sem)
    len_copy.start()
    for g in range(GROUPS):
        for copy in copies(g):
            copy.start()
    len_copy.wait()
    base = pos_ref[0]
    count = len_ref.shape[1]
    lengths = len_ref[...]
    high = lax.shift_right_logical(lengths, 4)
    low = lengths - high * 16
    both = jnp.concatenate(
        [jnp.broadcast_to(high, (8, count)), jnp.broadcast_to(low, (8, count))], axis=0
    ).astype(F32).astype(BF16)
    row = lax.broadcasted_iota(jnp.int32, (count, count), 0)
    col = lax.broadcasted_iota(jnp.int32, (count, count), 1)
    lower = jnp.where(col <= row, 1.0, 0.0).astype(BF16)
    sums = dot(lower, both, NT)
    ends = sums[:, 0:1] * 16.0 + sums[:, 8:9]
    tokens = (base + lax.broadcasted_iota(jnp.int32, (count, ROWS), 1)).astype(F32)
    starts = jnp.max(jnp.where(ends <= tokens, ends, 0.0), axis=0, keepdims=True)
    starts = starts - base.astype(F32)
    starts = jnp.concatenate([starts, starts], axis=1)
    start_ref[...] = jnp.broadcast_to(starts, (8, 2 * ROWS))
    key_at = lax.broadcasted_iota(jnp.int32, (ROWS, 2 * ROWS), 0)
    query_at = lax.broadcasted_iota(jnp.int32, (ROWS, 2 * ROWS), 1) & (ROWS - 1)
    seen = (key_at <= query_at) & (key_at.astype(F32) >= starts)

    def group(g, carry):
        for copy in copies(g):
            copy.wait()
        keys = kv_ref[:, span(g * DIM, DIM)]
        for p in range(PAIRS):
            pair = g * PAIRS + p
            first = pair * 2 * DIM
            deltas = []
            for h in range(2):
                cols = span(first + h * DIM, DIM)
                prod = g_ref[:, cols].astype(F32) * o_ref[:, cols].astype(F32)
                deltas.append(jnp.sum(prod.T, axis=0, keepdims=True))
            delta = jnp.concatenate(deltas, axis=1)
            delta_ref[pl.ds(pair, 1), :] = delta.astype(BF16).astype(F32)
            scores = dot(keys, stacked(q_ref, first, 2), NT)
            scores = jnp.where(seen, scores, FILL)
            top = jnp.max(scores, axis=0, keepdims=True)
            max_ref[pl.ds(pair, 1), :] = top
            sum_ref[pl.ds(pair, 1), :] = jnp.sum(
                jnp.exp2(scores * TO_BITS - top * TO_BITS), axis=0, keepdims=True
            )
        return carry

    lax.fori_loop(0, GROUPS, group, 0)


def far_kernel(
    start_ref, delta_ref, max_ref, sum_ref, q_ref, g_ref, kv2_ref, kv1_ref,
    out_ref, p1_ref, ds2_ref, bits_ref,
    bias_ref, p2_ref,
):
    key_at = lax.broadcasted_iota(jnp.int32, (2 * ROWS, ROWS), 0).astype(F32) - 2.0 * ROWS
    bias_ref[...] = jnp.where(key_at >= start_ref[0:1, :ROWS], 0.0, FILL)

    def group(g, carry):
        gcols = span(g * DIM, DIM)
        keys2 = kv2_ref[:, gcols]
        keys1 = kv1_ref[:, gcols]
        values2 = kv2_ref[:, span(WIDE + g * DIM, DIM)]
        bias2 = jnp.concatenate([bias_ref[:ROWS, :]] * 2, axis=1)
        bias1 = jnp.concatenate([bias_ref[ROWS:, :]] * 2, axis=1)
        for p in range(PAIRS):
            pair = g * PAIRS + p
            first = pair * 2 * DIM
            query = stacked(q_ref, first, 2)
            scores2 = dot(keys2, query, NT) + bias2
            scores1 = dot(keys1, query, NT) + bias1
            own_max = max_ref[pl.ds(pair, 1), :]
            top = jnp.maximum(
                jnp.max(jnp.maximum(scores2, scores1), axis=0, keepdims=True), own_max
            )
            bits = top * TO_BITS
            exps2 = jnp.exp2(scores2 * TO_BITS - bits)
            exps1 = jnp.exp2(scores1 * TO_BITS - bits)
            denom = jnp.sum(exps2 + exps1, axis=0, keepdims=True) + sum_ref[
                pl.ds(pair, 1), :
            ] * jnp.exp2(own_max * TO_BITS - bits)
            bits_ref[pl.ds(pair, 1), :] = bits + jnp.log2(denom)
            inverse = 1.0 / denom
            probs2 = exps2 * inverse
            cols = span(first, 2 * DIM)
            p1_ref[:, cols] = (exps1 * inverse).astype(BF16)
            p2_ref[:, pl.ds(p * 2 * DIM, 2 * DIM)] = probs2.astype(BF16)
            grads = dot(values2, stacked(g_ref, first, 2), NT)
            ds2_ref[:, cols] = (probs2 * (grads - delta_ref[pl.ds(pair, 1), :])).astype(BF16)
        head0 = g * GROUP_COLS
        dk = dot(ds2_ref[:, span(head0, GROUP_COLS)], stacked(q_ref, head0, PER_GROUP), NN)
        dv = dot(p2_ref[...], stacked(g_ref, head0, PER_GROUP), NN)
        out_ref[:, gcols] = (dk * SCALE).astype(BF16)
        out_ref[:, span(WIDE + g * DIM, DIM)] = dv.astype(BF16)
        return carry

    lax.fori_loop(0, GROUPS, group, 0)


def near_kernel(delta_ref, p1_ref, q_ref, g_ref, kv1_ref, after_ref, out_ref, ds1_ref):
    def group(g, carry):
        gcols = span(g * DIM, DIM)
        values = kv1_ref[:, span(WIDE + g * DIM, DIM)]
        for p in range(PAIRS):
            pair = g * PAIRS + p
            first = pair * 2 * DIM
            cols = span(first, 2 * DIM)
            grads = dot(values, stacked(g_ref, first, 2), NT)
            probs = p1_ref[:, cols].astype(F32)
            ds1_ref[:, cols] = (probs * (grads - delta_ref[pl.ds(pair, 1), :])).astype(BF16)
        head0 = g * GROUP_COLS
        wide = span(head0, GROUP_COLS)
        dk = dot(ds1_ref[:, wide], stacked(q_ref, head0, PER_GROUP), NN)
        dv = dot(p1_ref[:, wide], stacked(g_ref, head0, PER_GROUP), NN)
        out_ref[:, gcols] = (dk * SCALE).astype(BF16)
        out_ref[:, span(WIDE + g * DIM, DIM)] = dv.astype(BF16)
        return carry

    lax.fori_loop(0, GROUPS, group, 0)


def own_kernel(
    start_ref, delta_ref, bits_ref, q_ref, g_ref, kv_ref, kv2_ref, kv1_ref, ds2_ref, ds1_ref, after_ref,
    dq_hbm, out_ref,
    ds_ref, p_ref, dq_ref, sems,
):
    key_at = lax.broadcasted_iota(jnp.int32, (ROWS, 2 * ROWS), 0)
    query_at = lax.broadcasted_iota(jnp.int32, (ROWS, 2 * ROWS), 1) & (ROWS - 1)
    seen = (key_at <= query_at) & (key_at.astype(F32) >= start_ref[0:1, :])

    def copy(g):
        cols = span(g * GROUP_COLS, GROUP_COLS)
        return pltpu.make_async_copy(dq_ref.at[:, cols], dq_hbm.at[:, cols], sems.at[g])

    def group(g, carry):
        gcols = span(g * DIM, DIM)
        vcols = span(WIDE + g * DIM, DIM)
        keys = kv_ref[:, gcols]
        values = kv_ref[:, vcols]
        turned = jnp.concatenate([kv2_ref[:, gcols].T, kv1_ref[:, gcols].T, keys.T], axis=1)
        for p in range(PAIRS):
            pair = g * PAIRS + p
            first = pair * 2 * DIM
            cols = span(first, 2 * DIM)
            here = pl.ds(p * 2 * DIM, 2 * DIM)
            scores = dot(keys, stacked(q_ref, first, 2), NT)
            probs = jnp.exp2(
                jnp.where(seen, scores * TO_BITS - bits_ref[pl.ds(pair, 1), :], FILL)
            )
            grads = dot(values, stacked(g_ref, first, 2), NT)
            low = (probs * (grads - delta_ref[pl.ds(pair, 1), :])).astype(BF16)
            ds_ref[:, here] = low
            p_ref[:, here] = probs.astype(BF16)
            score_grads = jnp.concatenate([ds2_ref[:, cols], ds1_ref[:, cols], low], axis=0)
            turned_grad = dot(turned, score_grads, NN) * SCALE
            for h in range(2):
                dq_ref[:, span(first + h * DIM, DIM)] = (
                    turned_grad[:, h * DIM:(h + 1) * DIM].T.astype(BF16)
                )
        copy(g).start()
        head0 = g * GROUP_COLS
        dk = dot(ds_ref[...], stacked(q_ref, head0, PER_GROUP), NN)
        dv = dot(p_ref[...], stacked(g_ref, head0, PER_GROUP), NN)
        out_ref[:, gcols] = dk * SCALE
        out_ref[:, vcols] = dv
        return carry

    lax.fori_loop(0, GROUPS, group, 0)
    for g in range(GROUPS):
        copy(g).wait()


def sum_kernel(own_ref, far_ref, near_ref, dk_ref, dv_ref):
    for part, ref in ((0, dk_ref), (1, dv_ref)):
        cols = pl.ds(part * WIDE, WIDE)
        total = own_ref[:, cols] + far_ref[:, cols].astype(F32) + near_ref[:, cols].astype(F32)
        ref[...] = total.astype(BF16)


def call(body, name, flops, ins, outs, scratch=()):
    spaces = {"s": pltpu.SMEM, "v": VMEM, "a": pl.ANY, "h": pltpu.HBM}
    return pl.pallas_call(
        body,
        name=name,
        in_specs=[pl.BlockSpec(memory_space=spaces[space]) for space in ins],
        out_specs=[pl.BlockSpec(memory_space=spaces[space]) for space, _, _ in outs],
        out_shape=[jax.ShapeDtypeStruct(shape, dtype) for _, shape, dtype in outs],
        scratch_shapes=list(scratch),
        cost_estimate=pl.CostEstimate(flops=flops, transcendentals=0, bytes_accessed=1 << 20),
        compiler_params=pltpu.CompilerParams(vmem_limit_bytes=12 << 20),
    )


def on_device(queries, keys, values, attn_out, output_gradient, doc_lengths):
    contexts = lax.axis_size("ctx")
    halves = lax.axis_size("head")
    blocks = contexts * halves
    count = doc_lengths.shape[0]

    def shifted(array, by):
        place = lambda i: (i % halves) * contexts + i // halves
        pairs = [(place(i), place(i + by)) for i in range(blocks) if 0 <= i + by < blocks]
        return lax.ppermute(array, ("head", "ctx"), pairs)

    keys, values, queries, attn_out, output_gradient, lengths = (
        pltpu.with_memory_space_constraint(array, pltpu.HBM)
        for array in (keys, values, queries, attn_out, output_gradient, doc_lengths.reshape(1, -1))
    )
    base = ((lax.axis_index("ctx") * halves + lax.axis_index("head")) * ROWS).reshape(1)
    stat = ("v", (HEADS // 2, 2 * ROWS), F32)
    rows = ("v", (8, 2 * ROWS), F32)
    both = ("v", (ROWS, 2 * WIDE), BF16)
    full = ("v", (ROWS, FULL), BF16)
    narrow = ("v", (ROWS, WIDE), BF16)
    dma = pltpu.SemaphoreType.DMA
    (kv,) = call(pack_kernel, "pack", 1 << 20, "hh", [both], [dma((2,))])(keys, values)
    kv2 = shifted(kv, 2)
    kv1 = shifted(kv, 1)
    q, g, start, delta, own_max, own_sum = call(
        local_kernel, "local", 1 << 30, "shhhhv", [full, full, rows, stat, stat, stat],
        [VMEM((1, count), jnp.int32), VMEM((ROWS, FULL), BF16), dma((3, GROUPS)), dma],
    )(base, lengths, queries, output_gradient, attn_out, kv)
    far, p1, ds2, bits = call(
        far_kernel, "far", 2 << 30, "v" * 8, [both, full, full, stat],
        [VMEM((2 * ROWS, ROWS), F32), VMEM((ROWS, GROUP_COLS), BF16)],
    )(start, delta, own_max, own_sum, q, g, kv2, kv1)
    back2 = shifted(far, -2)
    near, ds1 = call(near_kernel, "near", 1 << 30, "vvvvva", [both, full])(delta, p1, q, g, kv1, far)
    back1 = shifted(near, -1)
    query_grad, own = call(
        own_kernel, "own", 4 << 30, "v" * 10 + "a",
        [("h", (ROWS, FULL), BF16), ("v", (ROWS, 2 * WIDE), F32)],
        [VMEM((ROWS, GROUP_COLS), BF16), VMEM((ROWS, GROUP_COLS), BF16), VMEM((ROWS, FULL), BF16), dma((GROUPS,))],
    )(start, delta, bits, q, g, kv, kv2, kv1, ds2, ds1, near)
    key_gradient, value_gradient = call(sum_kernel, "sum", 1 << 20, "vvv", [narrow, narrow])(
        own, back2, back1
    )
    return query_grad, key_gradient, value_gradient


def solution(mesh):
    tokens = P(("ctx", "head"), None)
    return jax.shard_map(
        on_device,
        mesh=mesh,
        in_specs=(tokens,) * 5 + (P(),),
        out_specs=(tokens,) * 3,
        check_vma=False,
    )
```

time: 98.5 us -> 39 us (0.40)
  the two profiles are of different devices: /device:TPU:257 before, /device:TPU:255 now
where the time goes in v1:
time: 39 us; the launch traced here: 38.8 us
  Pallas kernels  15.4 us (39%)
  starting transfers between devices  12.5 us (32%)
  waiting for transfers between devices  10.2 us (26%)
  between operations  0.72 us (2%)
    ppermute x4, starting transfers between devices, shifted(): return lax.ppermute(array, ('head', 'ctx'), pairs)  12.5 us
    ppermute x4, waiting for transfers between devices, shifted(): return lax.ppermute(array, ('head', 'ctx'), pairs)  10.2 us
    pallas_call x1, Pallas kernels, on_device(): call(far_kernel, 'far', 2 << 30, 'v' * 8, [both, full, full, stat], [VMEM...  3.97 us
    pallas_call x1, Pallas kernels, on_device(): call(local_kernel, 'local', 1 << 30, 'shhhhv', [full, full, rows, stat, s...  3.79 us
    pallas_call x1, Pallas kernels, on_device(): call(own_kernel, 'own', 4 << 30, 'v' * 10 + 'a', [('h', (ROWS, FULL), BF1...  3.62 us
    pallas_call x1, Pallas kernels, on_device(): call(near_kernel, 'near', 1 << 30, 'vvvvva', [both, full])  2.26 us
    pallas_call x1, Pallas kernels, on_device(): call(pack_kernel, 'pack', 1 << 20, 'hh', [both], [dma((2,))])(keys, values)  0.99 us
  transfers between devices with their start and end apart: 4, of which 3 were waited for; matrix products, arithmetic and copies ran while one was open for 0% of the time, Pallas kernels for 25%

profile of v1, /device:TPU:255, one launch (start us, length us, event | category | flops | bytes accessed | tf_op | source)
XLA Modules:
  0.0 38.8 jit_solution(1293948717430586279)
XLA Ops:
  0.6 1.0 %pack.1.kv_ref = bf16[128,1024]{1,0:T(8,128)(2,1)S(1)} custom-call(bf16[128,512]{1,0:T(8,128)(2,1)} %k_ref.1, bf16[128,512]{1,0:T(8,128)(2,1)} %v_ref.1), custom_call_target="tpu_custom_call" | custom-call | flops 1048576 | bytes 1048576 | tf_op jit(solution)/shard_map/pack/pallas_call | solution.py:280
  1.6 4.9 %collective-permute-start.1 = (bf16[128,1024]{1,0:T(8,128)(2,1)S(1)}, bf16[128,1024]{1,0:T(8,128)(2,1)S(1)}, u32[]{:S(2)}, u32[]{:S(2)}) collective-permute-start(bf16[128,1024]{1,0:T(8,128)(2,1)S(1)} %pack.1.kv_ref), channel_id=1, source_target_pairs={{0,256},{256,1},{1,257},{257,2},{2,258},{258,3},{3,259},{259,4},{4... | collective-permute-start | bytes 786440 | tf_op jit(solution)/shard_map/ppermute | solution.py:267
  6.5 3.1 %collective-permute-start = (bf16[128,1024]{1,0:T(8,128)(2,1)S(1)}, bf16[128,1024]{1,0:T(8,128)(2,1)S(1)}, u32[]{:S(2)}, u32[]{:S(2)}) collective-permute-start(bf16[128,1024]{1,0:T(8,128)(2,1)S(1)} %pack.1.kv_ref), channel_id=1, source_target_pairs={{0,1},{256,257},{1,2},{257,258},{2,3},{258,259},{3,4},{259,260},{4... | collective-permute-start | bytes 786440 | tf_op jit(solution)/shard_map/ppermute | solution.py:267
  9.7 3.8 %local.1 = (bf16[128,4096]{1,0:T(8,128)(2,1)S(1)}, bf16[128,4096]{1,0:T(8,128)(2,1)S(1)}, f32[8,256]{1,0:T(8,128)S(1)}, f32[16,256]{1,0:T(8,128)S(1)}, f32[16,256]{1,0:T(8,128)S(1)}, /*index=5*/f32[16,256]{1,0:T(8,128)S(1)}) custom-call(s32[1]{0:T(128)} %bitcast.pos_ref, s32[1,512]{1,0:T(1,128)} %bitcast.2, bf16[128,4096]{1,0:T(8,128)(2,1)} %q_hbm.1, ...), custom_call_target="tpu_custom_call" | custom-call | flops 1073741824 | bytes 1048576 | tf_op jit(solution)/shard_map/local/pallas_call | solution.py:283
  13.5 0.0 collective-permute-done.1.kv1_ref
  13.5 2.0 %collective-permute-done.kv2_ref = bf16[128,1024]{1,0:T(8,128)(2,1)S(1)} collective-permute-done((bf16[128,1024]{1,0:T(8,128)(2,1)S(1)}, bf16[128,1024]{1,0:T(8,128)(2,1)S(1)}, u32[]{:S(2)}, u32[]{:S(2)}) %collective-permute-start) | collective-permute-done | bytes 262176 | tf_op jit(solution)/shard_map/ppermute | solution.py:267
  15.4 4.0 %far.1 = (bf16[128,1024]{1,0:T(8,128)(2,1)S(1)}, bf16[128,4096]{1,0:T(8,128)(2,1)S(1)}, bf16[128,4096]{1,0:T(8,128)(2,1)S(1)}, f32[16,256]{1,0:T(8,128)S(1)}) custom-call(f32[8,256]{1,0:T(8,128)S(1)} %get-tuple-element.19.start_ref, f32[16,256]{1,0:T(8,128)S(1)} %get-tuple-element.20.delta_ref, f32[16,256]{1,0:T(8,128)S(1)} %get-tuple-element.21.max_ref, ...), custom_call_target="tpu_custom_call" | custom-call | flops 2147483648 | bytes 1048576 | tf_op jit(solution)/shard_map/far/pallas_call | solution.py:287
  19.4 1.9 %collective-permute-start.2 = (bf16[128,1024]{1,0:T(8,128)(2,1)S(1)}, bf16[128,1024]{1,0:T(8,128)(2,1)S(1)}, u32[]{:S(2)}, u32[]{:S(2)}) collective-permute-start(bf16[128,1024]{1,0:T(8,128)(2,1)S(1)} %get-tuple-element.28.after_ref), channel_id=1, source_target_pairs={{1,0},{257,256},{2,1},{258,257},{3,2},{259,258},{4,3},{260,259},{5... | collective-permute-start | bytes 786440 | tf_op jit(solution)/shard_map/ppermute | solution.py:267
  21.4 2.3 %near.1 = (bf16[128,1024]{1,0:T(8,128)(2,1)S(1)}, bf16[128,4096]{1,0:T(8,128)(2,1)S(1)}) custom-call(f32[16,256]{1,0:T(8,128)S(1)} %get-tuple-element.20.delta_ref, bf16[128,4096]{1,0:T(8,128)(2,1)S(1)} %get-tuple-element.27.p1_ref, bf16[128,4096]{1,0:T(8,128)(2,1)S(1)} %get-tuple-element.23.q_ref, bf16[128,4096]{1,0:T(8,128)(2,1)S(1)} %get-tuple-element.24.g_ref, ...), custom_call_target="tpu_custom_call" | custom-call | flops 1073741824 | bytes 1048576 | tf_op jit(solution)/shard_map/near/pallas_call | solution.py:292
  23.6 2.6 %collective-permute-start.3 = (bf16[128,1024]{1,0:T(8,128)(2,1)S(1)}, bf16[128,1024]{1,0:T(8,128)(2,1)S(1)}, u32[]{:S(2)}, u32[]{:S(2)}) collective-permute-start(bf16[128,1024]{1,0:T(8,128)(2,1)S(1)} %get-tuple-element.30.after_ref), channel_id=1, source_target_pairs={{256,0},{1,256},{257,1},{2,257},{258,2},{3,258},{259,3},{4,259},{2... | collective-permute-start | bytes 786440 | tf_op jit(solution)/shard_map/ppermute | solution.py:267
  26.2 3.6 %own.1 = (bf16[128,4096]{1,0:T(8,128)(2,1)}, f32[128,1024]{1,0:T(8,128)S(1)}) custom-call(f32[8,256]{1,0:T(8,128)S(1)} %get-tuple-element.19.start_ref, f32[16,256]{1,0:T(8,128)S(1)} %get-tuple-element.20.delta_ref, f32[16,256]{1,0:T(8,128)S(1)} %get-tuple-element.25.bits_ref, bf16[128,4096]{1,0:T(8,128)(2,1)S(1)} %get-tuple-element.23.q_ref, ...), custom_call_target="tpu_custom_call" | custom-call | flops 4294967296 | bytes 1048576 | tf_op jit(solution)/shard_map/own/pallas_call | solution.py:294
  29.8 5.1 %collective-permute-done.2.far_ref = bf16[128,1024]{1,0:T(8,128)(2,1)S(1)} collective-permute-done((bf16[128,1024]{1,0:T(8,128)(2,1)S(1)}, bf16[128,1024]{1,0:T(8,128)(2,1)S(1)}, u32[]{:S(2)}, u32[]{:S(2)}) %collective-permute-start.2) | collective-permute-done | bytes 262176 | tf_op jit(solution)/shard_map/ppermute | solution.py:267
  35.0 3.1 %collective-permute-done.3.near_ref = bf16[128,1024]{1,0:T(8,128)(2,1)S(1)} collective-permute-done((bf16[128,1024]{1,0:T(8,128)(2,1)S(1)}, bf16[128,1024]{1,0:T(8,128)(2,1)S(1)}, u32[]{:S(2)}, u32[]{:S(2)}) %collective-permute-start.3) | collective-permute-done | bytes 262176 | tf_op jit(solution)/shard_map/ppermute | solution.py:267
  38.0 0.8 %sum.1 = (bf16[128,512]{1,0:T(8,128)(2,1)}, bf16[128,512]{1,0:T(8,128)(2,1)}) custom-call(f32[128,1024]{1,0:T(8,128)S(1)} %get-tuple-element.32.own_ref, bf16[128,1024]{1,0:T(8,128)(2,1)S(1)} %collective-permute-done.2.far_ref, bf16[128,1024]{1,0:T(8,128)(2,1)S(1)} %collective-permute-done.3.near_ref), custom_call_target="tpu_custom_call" | custom-call | flops 1048576 | bytes 1048576 | tf_op jit(solution)/shard_map/sum/pallas_call | solution.py:299
Async XLA Ops:
  1.6 11.8 %collective-permute-start.1 = (bf16[128,1024]{1,0:T(8,128)(2,1)S(1)}, bf16[128,1024]{1,0:T(8,128)(2,1)S(1)}, u32[]{:S(2)}, u32[]{:S(2)}) collective-permute-start(bf16[128,1024]{1,0:T(8,128)(2,1)S(1)} %pack.1.kv_ref), channel_id=1, source_target_pairs={{0,256},{256,1},{1,257},{257,2},{2,258},{258,3},{3,259},{259,4},{4... | collective-permute-start | bytes 786440 | tf_op jit(solution)/shard_map/ppermute | solution.py:267
  6.5 8.9 %collective-permute-start = (bf16[128,1024]{1,0:T(8,128)(2,1)S(1)}, bf16[128,1024]{1,0:T(8,128)(2,1)S(1)}, u32[]{:S(2)}, u32[]{:S(2)}) collective-permute-start(bf16[128,1024]{1,0:T(8,128)(2,1)S(1)} %pack.1.kv_ref), channel_id=1, source_target_pairs={{0,1},{256,257},{1,2},{257,258},{2,3},{258,259},{3,4},{259,260},{4... | collective-permute-start | bytes 786440 | tf_op jit(solution)/shard_map/ppermute | solution.py:267
  19.4 15.6 %collective-permute-start.2 = (bf16[128,1024]{1,0:T(8,128)(2,1)S(1)}, bf16[128,1024]{1,0:T(8,128)(2,1)S(1)}, u32[]{:S(2)}, u32[]{:S(2)}) collective-permute-start(bf16[128,1024]{1,0:T(8,128)(2,1)S(1)} %get-tuple-element.28.after_ref), channel_id=1, source_target_pairs={{1,0},{257,256},{2,1},{258,257},{3,2},{259,258},{4,3},{260,259},{5... | collective-permute-start | bytes 786440 | tf_op jit(solution)/shard_map/ppermute | solution.py:267
  23.6 14.4 %collective-permute-start.3 = (bf16[128,1024]{1,0:T(8,128)(2,1)S(1)}, bf16[128,1024]{1,0:T(8,128)(2,1)S(1)}, u32[]{:S(2)}, u32[]{:S(2)}) collective-permute-start(bf16[128,1024]{1,0:T(8,128)(2,1)S(1)} %get-tuple-element.30.after_ref), channel_id=1, source_target_pairs={{256,0},{1,256},{257,1},{2,257},{258,2},{3,258},{259,3},{4,259},{2... | collective-permute-start | bytes 786440 | tf_op jit(solution)/shard_map/ppermute | solution.py:267

commit v2 on v1

--- a/solution.py
+++ b/solution.py
@@ -14,6 +14,7 @@
 WIDE = GROUPS * DIM
 FULL = HEADS * DIM
 GROUP_COLS = PER_GROUP * DIM
+CHUNK = 128
 SCALE = DIM ** (-0.5)
 LOG2E = 1.4426950408889634
 TO_BITS = SCALE * LOG2E
@@ -30,6 +31,8 @@
 
 
 def span(start, size):
+    if isinstance(start, int):
+        return pl.ds(start, size)
     return pl.ds(pl.multiple_of(start, DIM), size)
 
 
@@ -48,7 +51,7 @@
 
 def local_kernel(
     pos_ref, len_hbm, q_hbm, g_hbm, o_hbm, kv_ref,
-    q_ref, g_ref, start_ref, delta_ref, max_ref, sum_ref,
+    q_ref, g_ref, start_ref, delta_ref, bits_ref, sum_ref,
     len_ref, o_ref, sems, len_sem,
 ):
     def copies(g):
@@ -99,88 +102,146 @@
                 prod = g_ref[:, cols].astype(F32) * o_ref[:, cols].astype(F32)
                 deltas.append(jnp.sum(prod.T, axis=0, keepdims=True))
             delta = jnp.concatenate(deltas, axis=1)
-            delta_ref[pl.ds(pair, 1), :] = delta.astype(BF16).astype(F32)
+            here = pl.ds(p * 2 * DIM, 2 * DIM)
+            delta_ref[pl.ds(g, 1), here] = delta.astype(BF16).astype(F32)
             scores = dot(keys, stacked(q_ref, first, 2), NT)
             scores = jnp.where(seen, scores, FILL)
             top = jnp.max(scores, axis=0, keepdims=True)
-            max_ref[pl.ds(pair, 1), :] = top
-            sum_ref[pl.ds(pair, 1), :] = jnp.sum(
-                jnp.exp2(scores * TO_BITS - top * TO_BITS), axis=0, keepdims=True
+            bits = top * TO_BITS
+            bits_ref[pl.ds(g, 1), here] = bits
+            sum_ref[pl.ds(g, 1), here] = jnp.sum(
+                jnp.exp2(scores * TO_BITS - bits), axis=0, keepdims=True
             )
         return carry
 
-    lax.fori_loop(0, GROUPS, group, 0)
-
-
-def far_kernel(
-    start_ref, delta_ref, max_ref, sum_ref, q_ref, g_ref, kv2_ref, kv1_ref,
-    out_ref, p1_ref, ds2_ref, bits_ref,
-    bias_ref, p2_ref,
+    for g in range(GROUPS):
+        group(g, 0)
+
+
+def pair_cols(p):
+    return pl.ds(p * 2 * DIM, 2 * DIM)
+
+
+def pre_kernel(
+    start_ref, delta_ref, own_bits_ref, own_sum_ref, q_ref, g_ref, kv2_ref,
+    exps_ref, grads_ref, bits_ref, sum_ref,
+    bias_ref, score_ref,
 ):
-    key_at = lax.broadcasted_iota(jnp.int32, (2 * ROWS, ROWS), 0).astype(F32) - 2.0 * ROWS
-    bias_ref[...] = jnp.where(key_at >= start_ref[0:1, :ROWS], 0.0, FILL)
-
-    def group(g, carry):
-        gcols = span(g * DIM, DIM)
-        keys2 = kv2_ref[:, gcols]
-        keys1 = kv1_ref[:, gcols]
-        values2 = kv2_ref[:, span(WIDE + g * DIM, DIM)]
-        bias2 = jnp.concatenate([bias_ref[:ROWS, :]] * 2, axis=1)
-        bias1 = jnp.concatenate([bias_ref[ROWS:, :]] * 2, axis=1)
-        for p in range(PAIRS):
-            pair = g * PAIRS + p
-            first = pair * 2 * DIM
-            query = stacked(q_ref, first, 2)
-            scores2 = dot(keys2, query, NT) + bias2
-            scores1 = dot(keys1, query, NT) + bias1
-            own_max = max_ref[pl.ds(pair, 1), :]
-            top = jnp.maximum(
-                jnp.max(jnp.maximum(scores2, scores1), axis=0, keepdims=True), own_max
-            )
-            bits = top * TO_BITS
-            exps2 = jnp.exp2(scores2 * TO_BITS - bits)
-            exps1 = jnp.exp2(scores1 * TO_BITS - bits)
-            denom = jnp.sum(exps2 + exps1, axis=0, keepdims=True) + sum_ref[
-                pl.ds(pair, 1), :
-            ] * jnp.exp2(own_max * TO_BITS - bits)
-            bits_ref[pl.ds(pair, 1), :] = bits + jnp.log2(denom)
+    key_at = lax.broadcasted_iota(jnp.int32, (ROWS, 2 * ROWS), 0).astype(F32) - 2.0 * ROWS
+    bias_ref[...] = jnp.where(key_at >= start_ref[0:1, :], 0.0, FILL)
+    tops = {}
+
+    def scores(g):
+        keys = kv2_ref[:, span(g * DIM, DIM)]
+        values = kv2_ref[:, span(WIDE + g * DIM, DIM)]
+        for p in range(PAIRS):
+            first = g * GROUP_COLS + p * 2 * DIM
+            cols = span(first, 2 * DIM)
+            value = dot(keys, stacked(q_ref, first, 2), NT) + bias_ref[...]
+            score_ref[:, cols] = value
+            tops[g, p] = jnp.max(value, axis=0, keepdims=True)
+            grads = dot(values, stacked(g_ref, first, 2), NT)
+            grads_ref[:, cols] = grads - delta_ref[g:g + 1, pair_cols(p)]
+
+    def probs(g):
+        for p in range(PAIRS):
+            cols = span(g * GROUP_COLS + p * 2 * DIM, 2 * DIM)
+            here = pair_cols(p)
+            own_bits = own_bits_ref[g:g + 1, here]
+            bits = jnp.maximum(tops[g, p] * TO_BITS, own_bits)
+            bits_ref[g:g + 1, here] = bits
+            exps = jnp.exp2(score_ref[:, cols] * TO_BITS - bits)
+            exps_ref[:, cols] = exps
+            sum_ref[g:g + 1, here] = jnp.sum(exps, axis=0, keepdims=True) + own_sum_ref[
+                g:g + 1, here
+            ] * jnp.exp2(own_bits - bits)
+
+    scores(0)
+    for g in range(GROUPS):
+        if g + 1 < GROUPS:
+            scores(g + 1)
+        probs(g)
+
+
+def mid_kernel(
+    start_ref, far_bits_ref, far_sum_ref, exps_ref, grads_ref, q_ref, g_ref, kv1_ref,
+    out_ref, ds2_ref, p1_ref, bits_ref,
+    bias_ref, score_ref, p2_ref,
+):
+    key_at = lax.broadcasted_iota(jnp.int32, (ROWS, 2 * ROWS), 0).astype(F32) - 1.0 * ROWS
+    bias_ref[...] = jnp.where(key_at >= start_ref[0:1, :], 0.0, FILL)
+    tops = {}
+
+    def scores(g):
+        keys = kv1_ref[:, span(g * DIM, DIM)]
+        for p in range(PAIRS):
+            first = g * GROUP_COLS + p * 2 * DIM
+            value = dot(keys, stacked(q_ref, first, 2), NT) + bias_ref[...]
+            score_ref[:, span(first, 2 * DIM)] = value
+            tops[g, p] = jnp.max(value, axis=0, keepdims=True)
+
+    def probs(g):
+        for p in range(PAIRS):
+            first = g * GROUP_COLS + p * 2 * DIM
+            cols = span(first, 2 * DIM)
+            here = pair_cols(p)
+            far_bits = far_bits_ref[g:g + 1, here]
+            bits = jnp.maximum(tops[g, p] * TO_BITS, far_bits)
+            total = jnp.zeros((CHUNK, 2 * DIM), F32)
+            for r in range(0, ROWS, CHUNK):
+                exps = jnp.exp2(score_ref[r:r + CHUNK, cols] * TO_BITS - bits)
+                score_ref[r:r + CHUNK, cols] = exps
+                total = total + exps
+            scale = jnp.exp2(far_bits - bits)
+            denom = jnp.sum(total, axis=0, keepdims=True) + far_sum_ref[g:g + 1, here] * scale
             inverse = 1.0 / denom
-            probs2 = exps2 * inverse
-            cols = span(first, 2 * DIM)
-            p1_ref[:, cols] = (exps1 * inverse).astype(BF16)
-            p2_ref[:, pl.ds(p * 2 * DIM, 2 * DIM)] = probs2.astype(BF16)
-            grads = dot(values2, stacked(g_ref, first, 2), NT)
-            ds2_ref[:, cols] = (probs2 * (grads - delta_ref[pl.ds(pair, 1), :])).astype(BF16)
+            weight = scale * inverse
+            bits_ref[g:g + 1, here] = bits + jnp.log2(denom)
+            for r in range(0, ROWS, CHUNK):
+                value = exps_ref[r:r + CHUNK, cols] * weight
+                p2_ref[r:r + CHUNK, cols] = value.astype(BF16)
+                ds2_ref[r:r + CHUNK, cols] = (value * grads_ref[r:r + CHUNK, cols]).astype(BF16)
+                p1_ref[r:r + CHUNK, cols] = (score_ref[r:r + CHUNK, cols] * inverse).astype(BF16)
+
+    def sums(g):
         head0 = g * GROUP_COLS
-        dk = dot(ds2_ref[:, span(head0, GROUP_COLS)], stacked(q_ref, head0, PER_GROUP), NN)
-        dv = dot(p2_ref[...], stacked(g_ref, head0, PER_GROUP), NN)
-        out_ref[:, gcols] = (dk * SCALE).astype(BF16)
+        group_span = span(head0, GROUP_COLS)
+        dk = dot(ds2_ref[:, group_span], stacked(q_ref, head0, PER_GROUP), NN)
+        dv = dot(p2_ref[:, group_span], stacked(g_ref, head0, PER_GROUP), NN)
+        out_ref[:, span(g * DIM, DIM)] = (dk * SCALE).astype(BF16)
         out_ref[:, span(WIDE + g * DIM, DIM)] = dv.astype(BF16)
-        return carry
-
-    lax.fori_loop(0, GROUPS, group, 0)
+
+    scores(0)
+    for g in range(GROUPS):
+        if g + 1 < GROUPS:
+            scores(g + 1)
+        probs(g)
+        sums(g)
 
 
 def near_kernel(delta_ref, p1_ref, q_ref, g_ref, kv1_ref, after_ref, out_ref, ds1_ref):
-    def group(g, carry):
-        gcols = span(g * DIM, DIM)
+    def scores(g):
         values = kv1_ref[:, span(WIDE + g * DIM, DIM)]
         for p in range(PAIRS):
-            pair = g * PAIRS + p
-            first = pair * 2 * DIM
+            first = g * GROUP_COLS + p * 2 * DIM
             cols = span(first, 2 * DIM)
             grads = dot(values, stacked(g_ref, first, 2), NT)
             probs = p1_ref[:, cols].astype(F32)
-            ds1_ref[:, cols] = (probs * (grads - delta_ref[pl.ds(pair, 1), :])).astype(BF16)
+            ds1_ref[:, cols] = (probs * (grads - delta_ref[g:g + 1, pair_cols(p)])).astype(BF16)
+
+    def sums(g):
         head0 = g * GROUP_COLS
-        wide = span(head0, GROUP_COLS)
-        dk = dot(ds1_ref[:, wide], stacked(q_ref, head0, PER_GROUP), NN)
-        dv = dot(p1_ref[:, wide], stacked(g_ref, head0, PER_GROUP), NN)
-        out_ref[:, gcols] = (dk * SCALE).astype(BF16)
+        group_span = span(head0, GROUP_COLS)
+        dv = dot(p1_ref[:, group_span], stacked(g_ref, head0, PER_GROUP), NN)
+        dk = dot(ds1_ref[:, group_span], stacked(q_ref, head0, PER_GROUP), NN)
+        out_ref[:, span(g * DIM, DIM)] = (dk * SCALE).astype(BF16)
         out_ref[:, span(WIDE + g * DIM, DIM)] = dv.astype(BF16)
-        return carry
-
-    lax.fori_loop(0, GROUPS, group, 0)
+
+    scores(0)
+    for g in range(GROUPS):
+        if g + 1 < GROUPS:
+            scores(g + 1)
+        sums(g)
 
 
 def own_kernel(
@@ -209,10 +270,10 @@
             here = pl.ds(p * 2 * DIM, 2 * DIM)
             scores = dot(keys, stacked(q_ref, first, 2), NT)
             probs = jnp.exp2(
-                jnp.where(seen, scores * TO_BITS - bits_ref[pl.ds(pair, 1), :], FILL)
+                jnp.where(seen, scores * TO_BITS - bits_ref[pl.ds(g, 1), pair_cols(p)], FILL)
             )
             grads = dot(values, stacked(g_ref, first, 2), NT)
-            low = (probs * (grads - delta_ref[pl.ds(pair, 1), :])).astype(BF16)
+            low = (probs * (grads - delta_ref[pl.ds(g, 1), pair_cols(p)])).astype(BF16)
             ds_ref[:, here] = low
             p_ref[:, here] = probs.astype(BF16)
             score_grads = jnp.concatenate([ds2_ref[:, cols], ds1_ref[:, cols], low], axis=0)
@@ -229,16 +290,23 @@
         out_ref[:, vcols] = dv
         return carry
 
-    lax.fori_loop(0, GROUPS, group, 0)
+    for g in range(GROUPS):
+        group(g, 0)
     for g in range(GROUPS):
         copy(g).wait()
 
 
-def sum_kernel(own_ref, far_ref, near_ref, dk_ref, dv_ref):
-    for part, ref in ((0, dk_ref), (1, dv_ref)):
+def sum_kernel(own_ref, far_ref, near_ref, dk_hbm, dv_hbm, total_ref, sems):
+    copies = []
+    for part, ref in ((0, dk_hbm), (1, dv_hbm)):
         cols = pl.ds(part * WIDE, WIDE)
         total = own_ref[:, cols] + far_ref[:, cols].astype(F32) + near_ref[:, cols].astype(F32)
-        ref[...] = total.astype(BF16)
+        total_ref[:, cols] = total.astype(BF16)
+        copy = pltpu.make_async_copy(total_ref.at[:, cols], ref, sems.at[part])
+        copy.start()
+        copies.append(copy)
+    for copy in copies:
+        copy.wait()
 
 
 def call(body, name, flops, ins, outs, scratch=()):
@@ -271,32 +339,40 @@
         for array in (keys, values, queries, attn_out, output_gradient, doc_lengths.reshape(1, -1))
     )
     base = ((lax.axis_index("ctx") * halves + lax.axis_index("head")) * ROWS).reshape(1)
-    stat = ("v", (HEADS // 2, 2 * ROWS), F32)
+    stat = ("v", (8, GROUP_COLS), F32)
     rows = ("v", (8, 2 * ROWS), F32)
     both = ("v", (ROWS, 2 * WIDE), BF16)
     full = ("v", (ROWS, FULL), BF16)
-    narrow = ("v", (ROWS, WIDE), BF16)
+    narrow = ("h", (ROWS, WIDE), BF16)
     dma = pltpu.SemaphoreType.DMA
     (kv,) = call(pack_kernel, "pack", 1 << 20, "hh", [both], [dma((2,))])(keys, values)
     kv2 = shifted(kv, 2)
     kv1 = shifted(kv, 1)
-    q, g, start, delta, own_max, own_sum = call(
+    q, g, start, delta, own_bits, own_sum = call(
         local_kernel, "local", 1 << 30, "shhhhv", [full, full, rows, stat, stat, stat],
         [VMEM((1, count), jnp.int32), VMEM((ROWS, FULL), BF16), dma((3, GROUPS)), dma],
     )(base, lengths, queries, output_gradient, attn_out, kv)
-    far, p1, ds2, bits = call(
-        far_kernel, "far", 2 << 30, "v" * 8, [both, full, full, stat],
-        [VMEM((2 * ROWS, ROWS), F32), VMEM((ROWS, GROUP_COLS), BF16)],
-    )(start, delta, own_max, own_sum, q, g, kv2, kv1)
+    exact = ("v", (ROWS, FULL), F32)
+    bias = VMEM((ROWS, 2 * ROWS), F32)
+    exact_scratch = VMEM((ROWS, FULL), F32)
+    exps, grads, far_bits, far_sum = call(
+        pre_kernel, "pre", 1 << 30, "v" * 7, [exact, exact, stat, stat], [bias, exact_scratch]
+    )(start, delta, own_bits, own_sum, q, g, kv2)
+    far, ds2, p1, bits = call(
+        mid_kernel, "mid", 1 << 30, "v" * 8, [both, full, full, stat],
+        [bias, exact_scratch, VMEM((ROWS, FULL), BF16)],
+    )(start, far_bits, far_sum, exps, grads, q, g, kv1)
     back2 = shifted(far, -2)
-    near, ds1 = call(near_kernel, "near", 1 << 30, "vvvvva", [both, full])(delta, p1, q, g, kv1, far)
+    near, ds1 = call(near_kernel, "near", 1 << 30, "v" * 5 + "a", [both, full])(
+        delta, p1, q, g, kv1, far
+    )
     back1 = shifted(near, -1)
     query_grad, own = call(
         own_kernel, "own", 4 << 30, "v" * 10 + "a",
         [("h", (ROWS, FULL), BF16), ("v", (ROWS, 2 * WIDE), F32)],
         [VMEM((ROWS, GROUP_COLS), BF16), VMEM((ROWS, GROUP_COLS), BF16), VMEM((ROWS, FULL), BF16), dma((GROUPS,))],
     )(start, delta, bits, q, g, kv, kv2, kv1, ds2, ds1, near)
-    key_gradient, value_gradient = call(sum_kernel, "sum", 1 << 20, "vvv", [narrow, narrow])(
+    key_gradient, value_gradient = call(sum_kernel, "sum", 1 << 20, "vvv", [narrow, narrow], [VMEM((ROWS, 2 * WIDE), BF16), dma((2,))])(
         own, back2, back1
     )
     return query_grad, key_gradient, value_gradient

time: 39 us -> 36.1 us (0.926)
  Pallas kernels: 15.4 us -> 12.8 us
  waiting for transfers between devices: 10.2 us -> 9.18 us
  starting transfers between devices: 12.5 us -> 13.1 us
    pallas_call x3 -> x4, Pallas kernels: 6.98 us -> 5.06 us  [the longest x1 2.05 us: on_device(): call(mid_kernel, 'mid', 1 << 30, 'v' * 8, [both, full, full, stat], [bias...]
    ppermute x4, waiting for transfers between devices: 10.2 us -> 9.18 us  [shifted(): return lax.ppermute(array, ('head', 'ctx'), pairs)]
    ppermute x4, starting transfers between devices: 12.5 us -> 13.1 us  [shifted(): return lax.ppermute(array, ('head', 'ctx'), pairs)]
    pallas_call x1, Pallas kernels: 3.62 us -> 3.12 us  [on_device(): call(own_kernel, 'own', 4 << 30, 'v' * 10 + 'a', [('h', (ROWS, FULL), BF1...]
where the time goes in v2:
time: 36.1 us; the launch traced here: 35.9 us
  starting transfers between devices  13.1 us (36%)
  Pallas kernels  12.8 us (35%)
  waiting for transfers between devices  9.18 us (25%)
  between operations  0.72 us (2%)
    ppermute x4, starting transfers between devices, shifted(): return lax.ppermute(array, ('head', 'ctx'), pairs)  13.1 us
    ppermute x4, waiting for transfers between devices, shifted(): return lax.ppermute(array, ('head', 'ctx'), pairs)  9.18 us
    pallas_call x1, Pallas kernels, on_device(): call(local_kernel, 'local', 1 << 30, 'shhhhv', [full, full, rows, stat, s...  3.67 us
    pallas_call x1, Pallas kernels, on_device(): call(own_kernel, 'own', 4 << 30, 'v' * 10 + 'a', [('h', (ROWS, FULL), BF1...  3.12 us
    pallas_call x1, Pallas kernels, on_device(): call(mid_kernel, 'mid', 1 << 30, 'v' * 8, [both, full, full, stat], [bias...  2.05 us
    pallas_call x1, Pallas kernels, on_device(): call(near_kernel, 'near', 1 << 30, 'v' * 5 + 'a', [both, full])  1.14 us
    pallas_call x1, Pallas kernels, on_device(): call(pre_kernel, 'pre', 1 << 30, 'v' * 7, [exact, exact, stat, stat], [bi...  1.11 us
    pallas_call x1, Pallas kernels, on_device(): call(pack_kernel, 'pack', 1 << 20, 'hh', [both], [dma((2,))])(keys, values)  0.99 us
  transfers between devices with their start and end apart: 4, of which 3 were waited for; matrix products, arithmetic and copies ran while one was open for 0% of the time, Pallas kernels for 25%

profile of v2, /device:TPU:255, one launch (start us, length us, event | category | flops | bytes accessed | tf_op | source)
XLA Modules:
  0.0 35.9 jit_solution(14079120650731775839)
XLA Ops:
  0.6 1.0 %pack.1.kv_ref = bf16[128,1024]{1,0:T(8,128)(2,1)S(1)} custom-call(bf16[128,512]{1,0:T(8,128)(2,1)} %k_ref.1, bf16[128,512]{1,0:T(8,128)(2,1)} %v_ref.1), custom_call_target="tpu_custom_call" | custom-call | flops 1048576 | bytes 1048576 | tf_op jit(solution)/shard_map/pack/pallas_call | solution.py:348
  1.6 4.3 %collective-permute-start = (bf16[128,1024]{1,0:T(8,128)(2,1)S(1)}, bf16[128,1024]{1,0:T(8,128)(2,1)S(1)}, u32[]{:S(2)}, u32[]{:S(2)}) collective-permute-start(bf16[128,1024]{1,0:T(8,128)(2,1)S(1)} %pack.1.kv_ref), channel_id=1, source_target_pairs={{0,1},{256,257},{1,2},{257,258},{2,3},{258,259},{3,4},{259,260},{4... | collective-permute-start | bytes 786440 | tf_op jit(solution)/shard_map/ppermute | solution.py:335
  6.0 4.0 %collective-permute-start.1 = (bf16[128,1024]{1,0:T(8,128)(2,1)S(1)}, bf16[128,1024]{1,0:T(8,128)(2,1)S(1)}, u32[]{:S(2)}, u32[]{:S(2)}) collective-permute-start(bf16[128,1024]{1,0:T(8,128)(2,1)S(1)} %pack.1.kv_ref), channel_id=1, source_target_pairs={{0,256},{256,1},{1,257},{257,2},{2,258},{258,3},{3,259},{259,4},{4... | collective-permute-start | bytes 786440 | tf_op jit(solution)/shard_map/ppermute | solution.py:335
  9.9 3.7 %local.1 = (bf16[128,4096]{1,0:T(8,128)(2,1)S(1)}, bf16[128,4096]{1,0:T(8,128)(2,1)S(1)}, f32[8,256]{1,0:T(8,128)S(1)}, f32[8,1024]{1,0:T(8,128)S(1)}, f32[8,1024]{1,0:T(8,128)S(1)}, /*index=5*/f32[8,1024]{1,0:T(8,128)S(1)}) custom-call(s32[1]{0:T(128)} %bitcast.pos_ref, s32[1,512]{1,0:T(1,128)} %bitcast.2, bf16[128,4096]{1,0:T(8,128)(2,1)} %q_hbm.1, ...), custom_call_target="tpu_custom_call" | custom-call | flops 1073741824 | bytes 1048576 | tf_op jit(solution)/shard_map/local/pallas_call | solution.py:351
  13.6 0.0 collective-permute-done.kv2_ref
  13.6 1.1 %pre.1 = (f32[128,4096]{1,0:T(8,128)S(1)}, f32[128,4096]{1,0:T(8,128)S(1)}, f32[8,1024]{1,0:T(8,128)S(1)}, f32[8,1024]{1,0:T(8,128)S(1)}) custom-call(f32[8,256]{1,0:T(8,128)S(1)} %get-tuple-element.23.start_ref, f32[8,1024]{1,0:T(8,128)S(1)} %get-tuple-element.24.delta_ref, f32[8,1024]{1,0:T(8,128)S(1)} %get-tuple-element.25.own_bits_ref, ...), custom_call_target="tpu_custom_call" | custom-call | flops 1073741824 | bytes 1048576 | tf_op jit(solution)/shard_map/pre/pallas_call | solution.py:358
  14.7 0.1 collective-permute-done.1.kv1_ref
  14.9 2.0 %mid.1 = (bf16[128,1024]{1,0:T(8,128)(2,1)S(1)}, bf16[128,4096]{1,0:T(8,128)(2,1)S(1)}, bf16[128,4096]{1,0:T(8,128)(2,1)S(1)}, f32[8,1024]{1,0:T(8,128)S(1)}) custom-call(f32[8,256]{1,0:T(8,128)S(1)} %get-tuple-element.23.start_ref, f32[8,1024]{1,0:T(8,128)S(1)} %get-tuple-element.29.far_bits_ref, f32[8,1024]{1,0:T(8,128)S(1)} %get-tuple-element.30.far_sum_ref, ...), custom_call_target="tpu_custom_call" | custom-call | flops 1073741824 | bytes 1048576 | tf_op jit(solution)/shard_map/mid/pallas_call | solution.py:361
  16.9 2.1 %collective-permute-start.2 = (bf16[128,1024]{1,0:T(8,128)(2,1)S(1)}, bf16[128,1024]{1,0:T(8,128)(2,1)S(1)}, u32[]{:S(2)}, u32[]{:S(2)}) collective-permute-start(bf16[128,1024]{1,0:T(8,128)(2,1)S(1)} %get-tuple-element.36.after_ref), channel_id=1, source_target_pairs={{1,0},{257,256},{2,1},{258,257},{3,2},{259,258},{4,3},{260,259},{5... | collective-permute-start | bytes 786440 | tf_op jit(solution)/shard_map/ppermute | solution.py:335
  19.0 1.1 %near.1 = (bf16[128,1024]{1,0:T(8,128)(2,1)S(1)}, bf16[128,4096]{1,0:T(8,128)(2,1)S(1)}) custom-call(f32[8,1024]{1,0:T(8,128)S(1)} %get-tuple-element.24.delta_ref, bf16[128,4096]{1,0:T(8,128)(2,1)S(1)} %get-tuple-element.35.p1_ref, bf16[128,4096]{1,0:T(8,128)(2,1)S(1)} %get-tuple-element.27.q_ref, bf16[128,4096]{1,0:T(8,128)(2,1)S(1)} %get-tuple-element.28.g_ref, ...), custom_call_target="tpu_custom_call" | custom-call | flops 1073741824 | bytes 1048576 | tf_op jit(solution)/shard_map/near/pallas_call | solution.py:366
  20.1 2.8 %collective-permute-start.3 = (bf16[128,1024]{1,0:T(8,128)(2,1)S(1)}, bf16[128,1024]{1,0:T(8,128)(2,1)S(1)}, u32[]{:S(2)}, u32[]{:S(2)}) collective-permute-start(bf16[128,1024]{1,0:T(8,128)(2,1)S(1)} %get-tuple-element.38.after_ref), channel_id=1, source_target_pairs={{256,0},{1,256},{257,1},{2,257},{258,2},{3,258},{259,3},{4,259},{2... | collective-permute-start | bytes 786440 | tf_op jit(solution)/shard_map/ppermute | solution.py:335
  22.9 3.1 %own.1 = (bf16[128,4096]{1,0:T(8,128)(2,1)}, f32[128,1024]{1,0:T(8,128)S(1)}) custom-call(f32[8,256]{1,0:T(8,128)S(1)} %get-tuple-element.23.start_ref, f32[8,1024]{1,0:T(8,128)S(1)} %get-tuple-element.24.delta_ref, f32[8,1024]{1,0:T(8,128)S(1)} %get-tuple-element.33.bits_ref, bf16[128,4096]{1,0:T(8,128)(2,1)S(1)} %get-tuple-element.27.q_ref, ...), custom_call_target="tpu_custom_call" | custom-call | flops 4294967296 | bytes 1048576 | tf_op jit(solution)/shard_map/own/pallas_call | solution.py:370
  26.1 5.2 %collective-permute-done.2.far_ref = bf16[128,1024]{1,0:T(8,128)(2,1)S(1)} collective-permute-done((bf16[128,1024]{1,0:T(8,128)(2,1)S(1)}, bf16[128,1024]{1,0:T(8,128)(2,1)S(1)}, u32[]{:S(2)}, u32[]{:S(2)}) %collective-permute-start.2) | collective-permute-done | bytes 262176 | tf_op jit(solution)/shard_map/ppermute | solution.py:335
  31.3 3.8 %collective-permute-done.3.near_ref = bf16[128,1024]{1,0:T(8,128)(2,1)S(1)} collective-permute-done((bf16[128,1024]{1,0:T(8,128)(2,1)S(1)}, bf16[128,1024]{1,0:T(8,128)(2,1)S(1)}, u32[]{:S(2)}, u32[]{:S(2)}) %collective-permute-start.3) | collective-permute-done | bytes 262176 | tf_op jit(solution)/shard_map/ppermute | solution.py:335
  35.1 0.8 %sum.1 = (bf16[128,512]{1,0:T(8,128)(2,1)}, bf16[128,512]{1,0:T(8,128)(2,1)}) custom-call(f32[128,1024]{1,0:T(8,128)S(1)} %get-tuple-element.40.own_ref, bf16[128,1024]{1,0:T(8,128)(2,1)S(1)} %collective-permute-done.2.far_ref, bf16[128,1024]{1,0:T(8,128)(2,1)S(1)} %collective-permute-done.3.near_ref), custom_call_target="tpu_custom_call" | custom-call | flops 1048576 | bytes 1048576 | tf_op jit(solution)/shard_map/sum/pallas_call | solution.py:375
Async XLA Ops:
  1.6 12.0 %collective-permute-start = (bf16[128,1024]{1,0:T(8,128)(2,1)S(1)}, bf16[128,1024]{1,0:T(8,128)(2,1)S(1)}, u32[]{:S(2)}, u32[]{:S(2)}) collective-permute-start(bf16[128,1024]{1,0:T(8,128)(2,1)S(1)} %pack.1.kv_ref), channel_id=1, source_target_pairs={{0,1},{256,257},{1,2},{257,258},{2,3},{258,259},{3,4},{259,260},{4... | collective-permute-start | bytes 786440 | tf_op jit(solution)/shard_map/ppermute | solution.py:335
  6.0 8.9 %collective-permute-start.1 = (bf16[128,1024]{1,0:T(8,128)(2,1)S(1)}, bf16[128,1024]{1,0:T(8,128)(2,1)S(1)}, u32[]{:S(2)}, u32[]{:S(2)}) collective-permute-start(bf16[128,1024]{1,0:T(8,128)(2,1)S(1)} %pack.1.kv_ref), channel_id=1, source_target_pairs={{0,256},{256,1},{1,257},{257,2},{2,258},{258,3},{3,259},{259,4},{4... | collective-permute-start | bytes 786440 | tf_op jit(solution)/shard_map/ppermute | solution.py:335
  16.9 14.3 %collective-permute-start.2 = (bf16[128,1024]{1,0:T(8,128)(2,1)S(1)}, bf16[128,1024]{1,0:T(8,128)(2,1)S(1)}, u32[]{:S(2)}, u32[]{:S(2)}) collective-permute-start(bf16[128,1024]{1,0:T(8,128)(2,1)S(1)} %get-tuple-element.36.after_ref), channel_id=1, source_target_pairs={{1,0},{257,256},{2,1},{258,257},{3,2},{259,258},{4,3},{260,259},{5... | collective-permute-start | bytes 786440 | tf_op jit(solution)/shard_map/ppermute | solution.py:335
  20.1 15.0 %collective-permute-start.3 = (bf16[128,1024]{1,0:T(8,128)(2,1)S(1)}, bf16[128,1024]{1,0:T(8,128)(2,1)S(1)}, u32[]{:S(2)}, u32[]{:S(2)}) collective-permute-start(bf16[128,1024]{1,0:T(8,128)(2,1)S(1)} %get-tuple-element.38.after_ref), channel_id=1, source_target_pairs={{256,0},{1,256},{257,1},{2,257},{258,2},{3,258},{259,3},{4,259},{2... | collective-permute-start | bytes 786440 | tf_op jit(solution)/shard_map/ppermute | solution.py:335
